TPU v7x, 32 devices: a whole 2x2x4 slice. The times are simulated.
32 devices in a mesh: groups: 2 (over y), gx: 4 (over z), gy: 4 (over x, core).
Axes of the slice: x: 2, y: 2, z: 4, core: 2. Of those that a mesh axis runs over, the one named last changes fastest.
Arguments:
- thermal_deviation: float32 [32, 256, 512], P('groups', 'gy', 'gx'), parts along dimension 0, may hold values from -6 to 6
- brine_content: float32 [32, 256, 512], P('groups', 'gy', 'gx'), parts along dimension 0, may hold values from 0.2 to 2.4
- current_components: float32 [4, 16, 256, 512], P('groups', None, 'gy', 'gx'), parts along dimension 0, may hold values from -4 to 4
- sea_indicator: int32 [256, 512], P('gy', 'gx'), may hold values from 0 to 1, as said below
- flooded_layer_number: int32 [256, 512], P('gy', 'gx'), may hold values from 1 to 16
- footprint_square_metres: float32 [256, 512], P('gy', 'gx'), may hold values from 0.5 to 5
- rainfall_input: float32 [256, 512], P('gy', 'gx'), may hold values from -2 to 3.5
- seam_partner_index: int32 [512], P('gx'), may hold values from 0 to 511, as said below
Outputs:
- temperature_next: float32 [32, 256, 512], P('groups', 'gy', 'gx'), parts along dimension 0
- salinity_next: float32 [32, 256, 512], P('groups', 'gy', 'gx'), parts along dimension 0
There are 2 independent parts, one for each index of `groups`. A program takes and returns all parts, laid end to end along the dimension named above; an argument that names none is the same for every part. Nothing has to cross between parts.
Inputs may be any that keep to these rules, and one draw needn't show every extreme that they name: `sea_indicator`: at least one column is ocean. seam_partner_index[x] = (s - x) mod 512 for one s of each draw with s mod 128 = 127; the map is its own inverse and has no fixed point.
All inputs are finite; a program needn't handle non-finite values.
Results may differ from a plain program's by a relative error of at most 0.00002.
Values sent between devices are 32-bit elements; how exact they have to be, the bound alone decides.
A program may use at most 64 MiB of HBM per device.

v0:
```python
import jax
import jax.numpy as jnp
from jax import lax
from jax.sharding import PartitionSpec as P

time_step = 0.25
diffusivity = 0.5
vertical_mixing = 0.3
top_thickness = 0.5


def with_halo(cells, sides, width, closed):
    for axis, dim in sides:
        count = lax.axis_size(axis)
        ends = count if closed else count - 1
        head = lax.slice_in_dim(cells, 0, width, axis=dim)
        tail = lax.slice_in_dim(cells, cells.shape[dim] - width, cells.shape[dim], axis=dim)
        cells = jnp.concatenate(
            [
                lax.ppermute(tail, axis, [(i, (i + 1) % count) for i in range(ends)]),
                cells,
                lax.ppermute(head, axis, [((i + 1) % count, i) for i in range(ends)]),
            ],
            axis=dim,
        )
    return cells


def face_flux(near_cells, far_cells, face_speed, near_wet, far_wet):
    upwind = jnp.maximum(face_speed, 0.0) * near_cells + jnp.minimum(face_speed, 0.0) * far_cells
    return near_wet * far_wet * (upwind - diffusivity * (far_cells - near_cells))


def wet_from(depth_plane, layer_stack_number):
    level_index = jnp.arange(layer_stack_number, dtype=jnp.float32)
    return (level_index[:, None, None] < depth_plane[None]).astype(jnp.float32)


def split_tracer(block_planes, layer_stack_number):
    return block_planes[: 2 * layer_stack_number].reshape(
        (2, layer_stack_number) + block_planes.shape[1:]
    )


def shards(
    thermal_deviation,
    brine_content,
    current_components,
    sea_indicator,
    flooded_layer_number,
    footprint_square_metres,
    rainfall_input,
    seam_partner_index,
):
    layer_stack_number, parallel_total_number, meridian_total_number = thermal_deviation.shape
    stacked_layer_number = (sea_indicator * flooded_layer_number).astype(jnp.float32)
    wet_area = footprint_square_metres * sea_indicator.astype(jnp.float32)
    surface = brine_content[0]
    total_area, total_fresh, salt_fresh, salt_only = lax.psum(
        (
            jnp.sum(wet_area),
            jnp.sum(wet_area * rainfall_input),
            jnp.sum(wet_area * surface * rainfall_input),
            jnp.sum(wet_area * surface),
        ),
        ("gx", "gy"),
    )
    mean_fresh = total_fresh / total_area
    balanced = rainfall_input - mean_fresh
    total_salt = salt_fresh - mean_fresh * salt_only
    virtual = -surface * balanced + total_salt / total_area
    top_row = jnp.concatenate(
        [
            thermal_deviation[:, -1, :],
            brine_content[:, -1, :],
            current_components[1][:, -1, :],
            stacked_layer_number[-1:, :],
        ],
        axis=0,
    )
    gathered = lax.all_gather(top_row, "gx", axis=1, tiled=True)
    partner_row = jnp.take(gathered, seam_partner_index, axis=1)
    partner_fields = jnp.concatenate(
        [partner_row[: 2 * layer_stack_number], partner_row[3 * layer_stack_number :]], axis=0
    )
    partner_speed = partner_row[2 * layer_stack_number : 3 * layer_stack_number]
    is_top = lax.axis_index("gy") == lax.axis_size("gy") - 1
    planes = jnp.concatenate(
        [
            thermal_deviation,
            brine_content,
            current_components[0],
            current_components[1],
            stacked_layer_number[None],
        ],
        axis=0,
    )
    zonal_padded = with_halo(planes, (("gx", 2),), 1, True)
    meridional_padded = with_halo(planes, (("gy", 1),), 1, False)
    zonal_tracer = split_tracer(zonal_padded, layer_stack_number)
    zonal_wet = wet_from(zonal_padded[4 * layer_stack_number], layer_stack_number)
    zonal_near_speed = zonal_padded[2 * layer_stack_number : 3 * layer_stack_number][..., :-1]
    halo_top = jnp.concatenate(
        [
            meridional_padded[: 2 * layer_stack_number, -1, :],
            meridional_padded[4 * layer_stack_number :, -1, :],
        ],
        axis=0,
    )
    above_fields = jnp.where(is_top, partner_fields, halo_top)
    upper_tracer_cells = jnp.concatenate(
        [
            meridional_padded[: 2 * layer_stack_number, 1:-1, :],
            above_fields[: 2 * layer_stack_number, None, :],
        ],
        axis=1,
    )
    upper_depth = jnp.concatenate(
        [
            meridional_padded[4 * layer_stack_number, 1:-1, :],
            above_fields[2 * layer_stack_number][None, :],
        ],
        axis=0,
    )
    lower_cells = meridional_padded[:, :-1, :]
    lower_tracer = split_tracer(lower_cells, layer_stack_number)
    lower_wet = wet_from(lower_cells[4 * layer_stack_number], layer_stack_number)
    upper_tracer = split_tracer(upper_tracer_cells, layer_stack_number)
    upper_wet = wet_from(upper_depth, layer_stack_number)
    north_speed = lower_cells[3 * layer_stack_number : 4 * layer_stack_number]
    carried_quantity = jnp.stack([thermal_deviation, brine_content])
    wet_cells = wet_from(stacked_layer_number, layer_stack_number)
    zonal_flux = face_flux(
        zonal_tracer[..., :-1],
        zonal_tracer[..., 1:],
        zonal_near_speed,
        zonal_wet[..., :-1],
        zonal_wet[..., 1:],
    )
    fold_speed = 0.5 * (north_speed[:, -1, :] - partner_speed)
    last_speed = jnp.where(is_top, fold_speed, north_speed[:, -1, :])
    north_speed = jnp.concatenate([north_speed[:, :-1, :], last_speed[:, None, :]], axis=1)
    meridional_flux = face_flux(lower_tracer, upper_tracer, north_speed, lower_wet, upper_wet)
    vertical = (
        wet_cells[:-1]
        * wet_cells[1:]
        * vertical_mixing
        * (carried_quantity[:, :-1] - carried_quantity[:, 1:])
    )
    zero_layer = jnp.zeros_like(vertical[:, :1])
    from_above = jnp.concatenate([zero_layer, vertical], axis=1)
    to_below = jnp.concatenate([vertical, zero_layer], axis=1)
    tendency = time_step / footprint_square_metres * (
        zonal_flux[..., :-1]
        - zonal_flux[..., 1:]
        + meridional_flux[:, :, :-1]
        - meridional_flux[:, :, 1:]
    ) + time_step * (from_above - to_below)
    updated = carried_quantity + wet_cells * tendency
    surface_next = updated[1, 0] + time_step / top_thickness * virtual * wet_cells[0]
    salinity_next = jnp.concatenate([surface_next[None], updated[1, 1:]], axis=0)
    return (updated[0], salinity_next)


def solution(mesh):
    in_specs = (
        P("groups", "gy", "gx"),
        P("groups", "gy", "gx"),
        P("groups", None, "gy", "gx"),
        P("gy", "gx"),
        P("gy", "gx"),
        P("gy", "gx"),
        P("gy", "gx"),
        P("gx"),
    )
    out_specs = (P("groups", "gy", "gx"), P("groups", "gy", "gx"))
    return jax.shard_map(shards, mesh=mesh, in_specs=in_specs, out_specs=out_specs, check_vma=False)
```

profile of v0, /device:TPU:0, one launch (start us, length us, event | category | flops | bytes accessed | tf_op | source)
XLA Modules:
  0.0 111.4 jit_solution(16813490816440808588)
XLA Ops:
  0.6 2.3 %constant_dynamic-update-slice_fusion.2 = (f32[65,64,128]{2,0,1:T(8,128)S(1)}, f32[16,64,128]{2,0,1:T(8,128)}) fusion(f32[16,64,128]{2,1,0:T(8,128)} %param.8), kind=kLoop, calls=%fused_computation.82 | loop fusion | bytes 1572864
  3.1 1.1 %constant_dynamic-update-slice_fusion.1 = (f32[65,64,128]{2,0,1:T(8,128)S(1)}, f32[16,64,128]{2,0,1:T(8,128)}) fusion(f32[65,64,128]{2,0,1:T(8,128)S(1)} %get-tuple-element.22, f32[16,64,128]{2,1,0:T(8,128)S(1)} %copy-done.2), kind=kLoop, calls=%fused_computation.81 | loop fusion | bytes 1572864
  5.0 2.9 %fusion.24 = (f32[65,64,1]{2,0,1:T(8,128)}, f32[65,64,1]{2,0,1:T(8,128)}) fusion(f32[65,64,128]{2,0,1:T(8,128)S(1)} %dynamic-update-slice.4), kind=kLoop, calls=%fused_computation.87 | loop fusion | bytes 66560 | tf_op jit(solution)/shard_map/slice | solution.py:17
  7.9 3.1 %copy.160 = f32[65,64,1]{0,1,2:T(8,128)} copy(f32[65,64,1]{2,0,1:T(8,128)} %get-tuple-element.14) | data formatting | bytes 33280 | tf_op jit(solution)/shard_map/slice | solution.py:17
  11.0 3.1 %collective-permute-start = (f32[65,64,1]{0,1,2:T(8,128)}, f32[65,64,1]{0,1,2:T(8,128)}, u32[]{:S(2)}, u32[]{:S(2)}) collective-permute-start(f32[65,64,1]{0,1,2:T(8,128)} %copy.160), channel_id=1, source_target_pairs={{0,4},{4,8},{8,12},{12,0},{1,5},{5,9},{9,13},{13,1},{2,6},{6,10},{... | collective-permute-start | bytes 49928 | tf_op jit(solution)/shard_map/ppermute | solution.py:20
  14.0 3.1 %copy.161 = f32[65,64,1]{0,1,2:T(8,128)} copy(f32[65,64,1]{2,0,1:T(8,128)} %get-tuple-element.15) | data formatting | bytes 33280 | tf_op jit(solution)/shard_map/slice | solution.py:16
  17.1 2.1 %collective-permute-start.1 = (f32[65,64,1]{0,1,2:T(8,128)}, f32[65,64,1]{0,1,2:T(8,128)}, u32[]{:S(2)}, u32[]{:S(2)}) collective-permute-start(f32[65,64,1]{0,1,2:T(8,128)} %copy.161), channel_id=1, source_target_pairs={{4,0},{8,4},{12,8},{0,12},{5,1},{9,5},{13,9},{1,13},{6,2},{10,6},{... | collective-permute-start | bytes 49928 | tf_op jit(solution)/shard_map/ppermute | solution.py:22
  19.8 1.3 %collective-permute-start.2 = (f32[65,1,128]{2,0,1:T(8,128)}, f32[65,1,128]{2,0,1:T(8,128)}, u32[]{:S(2)}, u32[]{:S(2)}) collective-permute-start(f32[65,1,128]{2,0,1:T(8,128)} %get-tuple-element.17), channel_id=1, source_target_pairs={{1,0},{2,1},{3,2},{5,4},{6,5},{7,6},{9,8},{10,9},{11,10},{13,12},{... | collective-permute-start | bytes 99848 | tf_op jit(solution)/shard_map/ppermute | solution.py:22
  21.1 3.6 %collective-permute-start.3 = (f32[65,1,128]{2,0,1:T(8,128)}, f32[65,1,128]{2,0,1:T(8,128)}, u32[]{:S(2)}, u32[]{:S(2)}) collective-permute-start(f32[65,1,128]{2,0,1:T(8,128)} %get-tuple-element.16), channel_id=1, source_target_pairs={{0,1},{1,2},{2,3},{4,5},{5,6},{6,7},{8,9},{9,10},{10,11},{12,13},{... | collective-permute-start | bytes 99848 | tf_op jit(solution)/shard_map/ppermute | solution.py:20
  24.7 1.3 %copy.203 = f32[1,16,64,128]{3,1,2,0:T(8,128)S(1)} copy(f32[1,16,64,128]{3,2,1,0:T(8,128)} %copy-done.5) | data formatting | bytes 1048576
  27.3 1.1 pad_maximum_fusion.6
  30.6 13.3 %all_gather.3 = f32[49,512]{1,0:T(8,128)S(1)} all-gather(f32[49,128]{1,0:T(8,128)S(1)} %pad_maximum_fusion.11), channel_id=1, replica_groups=mesh['groups'=2,'gx'=4,'gy'=4] {'gx'}, dimensions={1}, use_global_device_ids=true | all-gather | bytes 125440 | tf_op jit(solution)/shard_map/all_gather | solution.py:81
  45.4 1.6 %gather_fusion = f32[128,49]{1,0:T(8,128)S(1)} fusion(f32[49,512]{0,1:T(8,128)} %copy.172, s32[1024]{0:T(1024)S(1)} %pad_clamp_fusion), kind=kCustom, calls=%fused_computation | custom fusion | bytes 50688 | tf_op jit(solution)/shard_map/jit(_take)/gather | solution.py:82
  47.7 2.0 %fusion.12 = f32[15,64,128]{2,1,0:T(8,128)} fusion(f32[16,64,128]{2,1,0:T(8,128)} %fusion.11), kind=kLoop, calls=%fused_computation.45 | loop fusion | flops 245760 | bytes 1474560 | tf_op jit(solution)/shard_map/mul | solution.py:145
  50.6 1.4 %select_bitcast_fusion = f32[49,128]{1,0:T(8,128)} fusion(f32[128,49]{0,1:T(8,128)} %copy.173, pred[128]{0:T(512)(128)(4,1)} %compare_and_fusion), kind=kLoop, calls=%fused_computation.68 | loop fusion | flops 6272 | bytes 50304 | tf_op jit(solution)/shard_map/jit(_take)/select_n | solution.py:82
  52.6 2.1 %fusion.7 = f32[2,15,64,128]{3,2,1,0:T(8,128)} fusion(f32[1,16,64,128]{3,2,1,0:T(8,128)S(1)} %bitcast.78, f32[1,16,64,128]{3,2,1,0:T(8,128)S(1)} %bitcast.76, f32[15,64,128]{2,1,0:T(8,128)} %fusion.12), kind=kLoop, calls=%fused_computation.26 | loop fusion | flops 983040 | bytes 2523136 | tf_op jit(solution)/shard_map/mul | solution.py:145
  55.4 30.3 %all-reduce.2 = (f32[]{:T(128)}, f32[]{:T(128)}, f32[]{:T(128)}, f32[]{:T(128)}) all-reduce(f32[]{:T(128)} %get-tuple-element.3, f32[]{:T(128)} %get-tuple-element.4, f32[]{:T(128)} %get-tuple-element.5, f32[]{:T(128)} %get-tuple-element.2), channel_id=1, replica_groups=mesh['groups'=2,'gx'=4,'gy'=4] {'gx','gy'}, use_global_device_ids=true, to_apply=%region_5.0 | all-reduce | flops 4 | bytes 32 | tf_op jit(solution)/shard_map/psum | solution.py:59
  88.9 3.0 %copy.162 = f32[65,64,1]{2,0,1:T(8,128)} copy(f32[65,64,1]{0,1,2:T(8,128)} %collective-permute-done) | data formatting | bytes 33280 | tf_op jit(solution)/shard_map/ppermute | solution.py:20
  91.9 3.0 %copy.163 = f32[65,64,1]{2,0,1:T(8,128)} copy(f32[65,64,1]{0,1,2:T(8,128)} %collective-permute-done.1) | data formatting | bytes 33280 | tf_op jit(solution)/shard_map/ppermute | solution.py:22
  94.9 1.5 %pad_maximum_fusion.8 = f32[1,64,130]{2,0,1:T(1,128)S(1)} fusion(f32[65,64,1]{2,0,1:T(8,128)} %copy.163, f32[65,64,128]{2,0,1:T(8,128)S(1)} %dynamic-update-slice.4, f32[65,64,1]{2,0,1:T(8,128)} %copy.162), kind=kLoop, calls=%fused_computation.48 | loop fusion | flops 16640 | bytes 2196480 | tf_op jit(solution)/shard_map/slice | solution.py:101
  97.5 0.9 pad_maximum_fusion
  99.2 1.2 %copy.167 = f32[32,64,130]{2,1,0:T(8,128)S(1)} copy(f32[32,64,130]{2,0,1:T(8,128)S(1)} %pad_maximum_fusion) | data formatting | bytes 2129920 | tf_op jit(solution)/shard_map/slice | solution.py:40
  101.8 1.1 subtract_multiply_fusion
  106.6 0.9 pad_maximum_fusion.4
  (85 shorter events, 20.0 us)
Async XLA Ops:
  0.6 2.3 %copy-start.8 = (f32[2,16,64,128]{3,2,1,0:T(8,128)S(1)}, f32[2,16,64,128]{3,2,1,0:T(8,128)}, u32[]{:S(2)}) copy-start(f32[2,16,64,128]{3,2,1,0:T(8,128)} %param.10) | copy-start | bytes 3145732
  0.6 2.4 %copy-start.2 = (f32[16,64,128]{2,1,0:T(8,128)S(1)}, f32[16,64,128]{2,1,0:T(8,128)}, u32[]{:S(2)}) copy-start(f32[16,64,128]{2,1,0:T(8,128)} %param.9) | copy-start | bytes 1572868
  3.0 1.8 %copy-start.5 = (f32[1,16,64,128]{3,2,1,0:T(8,128)}, f32[1,16,64,128]{3,2,1,0:T(8,128)S(1)}, u32[]{:S(2)}) copy-start(f32[1,16,64,128]{3,2,1,0:T(8,128)S(1)} %get-tuple-element.19) | copy-start | bytes 1572868
  3.0 1.8 %copy-start.11 = (s32[64,128]{1,0:T(8,128)S(1)}, s32[64,128]{1,0:T(8,128)}, u32[]{:S(2)}) copy-start(s32[64,128]{1,0:T(8,128)} %param.11) | copy-start | bytes 98308
  3.0 1.8 %copy-start.13 = (s32[64,128]{1,0:T(8,128)S(1)}, s32[64,128]{1,0:T(8,128)}, u32[]{:S(2)}) copy-start(s32[64,128]{1,0:T(8,128)} %param.12) | copy-start | bytes 98308
  11.0 15.1 %copy-start.14 = (s32[128]{0:T(128)S(1)}, s32[128]{0:T(128)}, u32[]{:S(2)}) copy-start(s32[128]{0:T(128)} %param.15) | copy-start | bytes 1540
  11.0 16.3 %copy-start.3 = (f32[16,64,128]{2,1,0:T(8,128)S(1)}, f32[16,64,128]{2,1,0:T(8,128)}, u32[]{:S(2)}) copy-start(f32[16,64,128]{2,1,0:T(8,128)} %param.8) | copy-start | bytes 1572868
  11.0 77.9 %collective-permute-start = (f32[65,64,1]{0,1,2:T(8,128)}, f32[65,64,1]{0,1,2:T(8,128)}, u32[]{:S(2)}, u32[]{:S(2)}) collective-permute-start(f32[65,64,1]{0,1,2:T(8,128)} %copy.160), channel_id=1, source_target_pairs={{0,4},{4,8},{8,12},{12,0},{1,5},{5,9},{9,13},{13,1},{2,6},{6,10},{... | collective-permute-start | bytes 49928 | tf_op jit(solution)/shard_map/ppermute | solution.py:20
  17.1 74.8 %collective-permute-start.1 = (f32[65,64,1]{0,1,2:T(8,128)}, f32[65,64,1]{0,1,2:T(8,128)}, u32[]{:S(2)}, u32[]{:S(2)}) collective-permute-start(f32[65,64,1]{0,1,2:T(8,128)} %copy.161), channel_id=1, source_target_pairs={{4,0},{8,4},{12,8},{0,12},{5,1},{9,5},{13,9},{1,13},{6,2},{10,6},{... | collective-permute-start | bytes 49928 | tf_op jit(solution)/shard_map/ppermute | solution.py:22
  19.8 83.1 %collective-permute-start.2 = (f32[65,1,128]{2,0,1:T(8,128)}, f32[65,1,128]{2,0,1:T(8,128)}, u32[]{:S(2)}, u32[]{:S(2)}) collective-permute-start(f32[65,1,128]{2,0,1:T(8,128)} %get-tuple-element.17), channel_id=1, source_target_pairs={{1,0},{2,1},{3,2},{5,4},{6,5},{7,6},{9,8},{10,9},{11,10},{13,12},{... | collective-permute-start | bytes 99848 | tf_op jit(solution)/shard_map/ppermute | solution.py:22
  21.1 83.2 %collective-permute-start.3 = (f32[65,1,128]{2,0,1:T(8,128)}, f32[65,1,128]{2,0,1:T(8,128)}, u32[]{:S(2)}, u32[]{:S(2)}) collective-permute-start(f32[65,1,128]{2,0,1:T(8,128)} %get-tuple-element.16), channel_id=1, source_target_pairs={{0,1},{1,2},{2,3},{4,5},{5,6},{6,7},{8,9},{9,10},{10,11},{12,13},{... | collective-permute-start | bytes 99848 | tf_op jit(solution)/shard_map/ppermute | solution.py:20
  26.1 3.8 %copy-start.9 = (f32[1,16,64,128]{3,1,2,0:T(8,128)}, f32[1,16,64,128]{3,1,2,0:T(8,128)S(1)}, u32[]{:S(2)}) copy-start(f32[1,16,64,128]{3,1,2,0:T(8,128)S(1)} %copy.203) | copy-start | bytes 1572868
  47.7 7.0 %copy-start.10 = (f32[64,128]{1,0:T(8,128)S(1)}, f32[64,128]{1,0:T(8,128)}, u32[]{:S(2)}) copy-start(f32[64,128]{1,0:T(8,128)} %param.14) | copy-start | bytes 98308
  94.9 1.8 %copy-start = (f32[65,64,1]{2,0,1:T(8,128)S(1)}, f32[65,64,1]{2,0,1:T(8,128)}, u32[]{:S(2)}) copy-start(f32[65,64,1]{2,0,1:T(8,128)} %copy.162) | copy-start | bytes 49924
  94.9 2.5 %copy-start.1 = (f32[65,64,1]{2,0,1:T(8,128)S(1)}, f32[65,64,1]{2,0,1:T(8,128)}, u32[]{:S(2)}) copy-start(f32[65,64,1]{2,0,1:T(8,128)} %copy.163) | copy-start | bytes 49924
  101.8 2.5 %slice-start = ((f32[49,128]{1,0:T(8,128)}), f32[32,128]{1,0:T(8,128)S(1)}, s32[]{:S(2)}) async-start(f32[49,128]{1,0:T(8,128)} %select_bitcast_fusion), calls=%async_computation | async-start | bytes 32768 | tf_op jit(solution)/shard_map/slice | solution.py:84
  101.8 2.5 %slice-start.1 = ((f32[49,128]{1,0:T(8,128)}), f32[1,128]{1,0:T(1,128)S(1)}, s32[]{:S(2)}) async-start(f32[49,128]{1,0:T(8,128)} %select_bitcast_fusion), calls=%async_computation.1 | async-start | bytes 1024 | tf_op jit(solution)/shard_map/slice | solution.py:84
  104.3 1.1 copy-start.12
  106.4 1.2 %copy-start.6 = (f32[32,64,128]{2,1,0:T(8,128)S(1)}, f32[32,64,128]{2,1,0:T(8,128)}, u32[]{:S(2)}) copy-start(f32[32,64,128]{2,1,0:T(8,128)} %pad_maximum_fusion.6) | copy-start | bytes 3145732
  106.4 1.2 %slice-start.2 = ((f32[33,128]{1,0:T(8,128)}), f32[32,128]{1,0:T(8,128)S(1)}, s32[]{:S(2)}) async-start(f32[33,128]{1,0:T(8,128)} %copy-done.12), calls=%async_computation.2 | async-start | bytes 32768 | tf_op jit(solution)/shard_map/slice | solution.py:114
  107.6 1.0 copy-start.4
  107.6 1.4 %copy-start.7 = (f32[2,15,64,128]{3,2,1,0:T(8,128)S(1)}, f32[2,15,64,128]{3,2,1,0:T(8,128)}, u32[]{:S(2)}) copy-start(f32[2,15,64,128]{3,2,1,0:T(8,128)} %fusion.7) | copy-start | bytes 2949124
where the time goes:
time: 112 us; the launch traced here: 111 us
  blocking collectives  43.6 us (39%)
  local copies, waits for them, and re-layouts  32.9 us (29%)
  other arithmetic  20.6 us (18%)
  starting transfers between devices  10.1 us (9%)
  between operations  4.18 us (4%)
    psum x1, blocking collectives, shards(): lax.psum((jnp.sum(wet_area), jnp.sum(wet_area * rainfall_input), jnp.sum(...  30.3 us
    all_gather x1, blocking collectives, shards(): gathered = lax.all_gather(top_row, 'gx', axis=1, tiled=True)  13.3 us
    unnamed x37, local copies, waits for them, and re-layouts  7.21 us
    ppermute x2, starting transfers between devices, with_halo(): lax.ppermute(tail, axis, [(i, (i + 1) % count) for i in range(ends)])  6.7 us
    slice x3, local copies, waits for them, and re-layouts, with_halo(): lax.slice_in_dim(cells, cells.shape[dim] - width, cells.shape[dim], axis=...  6.57 us
    mul x2, other arithmetic, shards(): wet_cells[:-1] * wet_cells[1:] * vertical_mixing  4.14 us
    ppermute x2, starting transfers between devices, with_halo(): lax.ppermute(head, axis, [((i + 1) % count, i) for i in range(ends)])  3.37 us
    slice x1, local copies, waits for them, and re-layouts, with_halo(): head = lax.slice_in_dim(cells, 0, width, axis=dim)  3.07 us
  transfers between devices with their start and end apart: 4, of which 0 were waited for; matrix products, arithmetic and copies ran while one was open for 32% of the time, Pallas kernels for 0%

commit v1 on v0

--- a/solution.py
+++ b/solution.py
@@ -7,6 +7,17 @@
 diffusivity = 0.5
 vertical_mixing = 0.3
 top_thickness = 0.5
+
+
+def collect(value, axis, dim):
+    ways = lax.axis_size(axis)
+    pieces = [value]
+    for far in range(1, ways):
+        pieces.append(
+            lax.ppermute(pieces[far - 1], axis, [(d, (d - 1) % ways) for d in range(ways)])
+        )
+    line = jnp.concatenate(pieces, axis=dim)
+    return jnp.roll(line, lax.axis_index(axis) * value.shape[dim], axis=dim)
 
 
 def with_halo(cells, sides, width, closed):
@@ -78,7 +89,7 @@
         ],
         axis=0,
     )
-    gathered = lax.all_gather(top_row, "gx", axis=1, tiled=True)
+    gathered = collect(top_row, "gx", 1)
     partner_row = jnp.take(gathered, seam_partner_index, axis=1)
     partner_fields = jnp.concatenate(
         [partner_row[: 2 * layer_stack_number], partner_row[3 * layer_stack_number :]], axis=0

time: 112 us -> 93.3 us (0.83)
  blocking collectives: 43.6 us -> 34.3 us
  other arithmetic: 20.6 us -> 12.4 us
  local copies, waits for them, and re-layouts: 32.9 us -> 26.6 us
  waiting for transfers between devices: 0.01 us -> 3.08 us
  starting transfers between devices: 10.1 us -> 11.9 us
    all_gather x1 -> x0, blocking collectives: 13.3 us -> none  [shards(): gathered = lax.all_gather(top_row, 'gx', axis=1, tiled=True)]
    ppermute x0 -> x3, starting transfers between devices: none -> 6.22 us  [collect(): lax.ppermute(pieces[far - 1], axis, [(d, (d - 1) % ways) for d in range(w...]
    psum x1, blocking collectives: 30.3 us -> 34.3 us  [shards(): lax.psum((jnp.sum(wet_area), jnp.sum(wet_area * rainfall_input), jnp.sum(...]
    ppermute x0 -> x3, waiting for transfers between devices: none -> 3.07 us  [collect(): lax.ppermute(pieces[far - 1], axis, [(d, (d - 1) % ways) for d in range(w...]
    mul x2, other arithmetic: 4.14 us -> 1.15 us  [shards(): wet_cells[:-1] * wet_cells[1:] * vertical_mixing]
    ppermute x2, starting transfers between devices: 6.7 us -> 3.98 us  [with_halo(): lax.ppermute(tail, axis, [(i, (i + 1) % count) for i in range(ends)])]
    slice x2 -> x1, other arithmetic: 2.16 us -> 0.05 us  [shards(): north_speed[:, :-1, :]]
    squeeze x3 -> x1, local copies, waits for them, and re-layouts: 2.12 us -> 0.04 us  [shards(): current_components[1]]
  transfers between devices with their start and end apart: 4 -> 7, of which waited for: 0 -> 2; matrix products, arithmetic and copies ran while one was open for 32% -> 31% of each run, Pallas kernels for 0% -> 0%
where the time goes in v1:
time: 93.3 us; the launch traced here: 92.8 us
  blocking collectives  34.3 us (37%)
  local copies, waits for them, and re-layouts  26.6 us (29%)
  other arithmetic  12.4 us (13%)
  starting transfers between devices  11.9 us (13%)
  between operations  4.38 us (5%)
  waiting for transfers between devices  3.08 us (3%)
    psum x1, blocking collectives, shards(): lax.psum((jnp.sum(wet_area), jnp.sum(wet_area * rainfall_input), jnp.sum(...  34.3 us
    unnamed x44, local copies, waits for them, and re-layouts  6.3 us
    ppermute x3, starting transfers between devices, collect(): lax.ppermute(pieces[far - 1], axis, [(d, (d - 1) % ways) for d in range(w...  6.22 us
    slice x2, local copies, waits for them, and re-layouts, with_halo(): lax.slice_in_dim(cells, cells.shape[dim] - width, cells.shape[dim], axis=...  6.16 us
    ppermute x2, starting transfers between devices, with_halo(): lax.ppermute(tail, axis, [(i, (i + 1) % count) for i in range(ends)])  3.98 us
    ppermute x1, local copies, waits for them, and re-layouts, with_halo(): lax.ppermute(head, axis, [((i + 1) % count, i) for i in range(ends)])  3.78 us
    ppermute x1, local copies, waits for them, and re-layouts, with_halo(): lax.ppermute(tail, axis, [(i, (i + 1) % count) for i in range(ends)])  3.74 us
    concatenate x2, other arithmetic, with_halo(): jnp.concatenate([lax.ppermute(tail, axis, [(i, (i + 1) % count) for i in...  3.71 us
  transfers between devices with their start and end apart: 7, of which 2 were waited for; matrix products, arithmetic and copies ran while one was open for 31% of the time, Pallas kernels for 0%

profile of v1, /device:TPU:0, one launch (start us, length us, event | category | flops | bytes accessed | tf_op | source)
XLA Modules:
  0.0 92.8 jit_solution(832288617540467360)
XLA Ops:
  0.7 1.2 %constant_dynamic-update-slice_fusion.2 = f32[65,64,128]{2,1,0:T(8,128)S(1)} fusion(f32[16,64,128]{2,1,0:T(8,128)} %param.8), kind=kLoop, calls=%fused_computation.68 | loop fusion | bytes 1048576
  1.9 1.2 %constant_dynamic-update-slice_fusion.1 = f32[65,64,128]{2,1,0:T(8,128)S(1)} fusion(f32[65,64,128]{2,1,0:T(8,128)S(1)} %constant_dynamic-update-slice_fusion.2, f32[16,64,128]{2,1,0:T(8,128)} %param.9), kind=kLoop, calls=%fused_computation.67 | loop fusion | bytes 1048576
  3.2 2.4 %collective-permute-start.6 = (f32[65,1,128]{2,1,0:T(1,128)S(1)}, f32[65,1,128]{2,1,0:T(1,128)S(1)}, u32[]{:S(2)}, u32[]{:S(2)}) collective-permute-start(f32[65,1,128]{2,1,0:T(1,128)S(1)} %get-tuple-element.17), channel_id=1, source_target_pairs={{0,1},{1,2},{2,3},{4,5},{5,6},{6,7},{8,9},{9,10},{10,11},{12,13},{... | collective-permute-start | bytes 99848 | tf_op jit(solution)/shard_map/ppermute | solution.py:31
  6.4 4.4 %collective-permute-start.2 = (f32[49,128]{1,0:T(8,128)}, f32[49,128]{1,0:T(8,128)S(1)}, u32[]{:S(2)}, u32[]{:S(2)}) collective-permute-start(f32[49,128]{1,0:T(8,128)} %get-tuple-element.22), channel_id=1, source_target_pairs={{0,12},{4,0},{8,4},{12,8},{1,13},{5,1},{9,5},{13,9},{2,14},{6,2},{... | collective-permute-start | bytes 75272 | tf_op jit(solution)/shard_map/ppermute | solution.py:17
  10.8 1.3 %collective-permute-start.5 = (f32[65,1,128]{2,1,0:T(1,128)S(1)}, f32[65,1,128]{2,1,0:T(1,128)}, u32[]{:S(2)}, u32[]{:S(2)}) collective-permute-start(f32[65,1,128]{2,1,0:T(1,128)S(1)} %get-tuple-element.16), channel_id=1, source_target_pairs={{1,0},{2,1},{3,2},{5,4},{6,5},{7,6},{9,8},{10,9},{11,10},{13,12},{... | collective-permute-start | bytes 99848 | tf_op jit(solution)/shard_map/ppermute | solution.py:33
  12.1 2.8 %fusion.23 = (f32[65,64,1]{2,1,0:T(8,128)}, f32[65,64,1]{2,1,0:T(8,128)}) fusion(f32[65,64,128]{2,1,0:T(8,128)S(1)} %get-tuple-element.12), kind=kLoop, calls=%fused_computation.89 | loop fusion | bytes 66560 | tf_op jit(solution)/shard_map/slice | solution.py:28
  14.9 2.8 %copy.92 = f32[65,64,1]{0,1,2:T(8,128)S(1)} copy(f32[65,64,1]{2,1,0:T(8,128)} %get-tuple-element.15) | data formatting | bytes 33280 | tf_op jit(solution)/shard_map/slice | solution.py:27
  18.2 3.3 %copy.91 = f32[65,64,1]{0,1,2:T(8,128)} copy(f32[65,64,1]{2,1,0:T(8,128)} %get-tuple-element.14) | data formatting | bytes 33280 | tf_op jit(solution)/shard_map/slice | solution.py:28
  21.5 1.6 %collective-permute-start = (f32[65,64,1]{0,1,2:T(8,128)}, f32[65,64,1]{0,1,2:T(8,128)}, u32[]{:S(2)}, u32[]{:S(2)}) collective-permute-start(f32[65,64,1]{0,1,2:T(8,128)} %copy.91), channel_id=1, source_target_pairs={{0,4},{4,8},{8,12},{12,0},{1,5},{5,9},{9,13},{13,1},{2,6},{6,10},{... | collective-permute-start | bytes 49928 | tf_op jit(solution)/shard_map/ppermute | solution.py:31
  23.1 1.1 %pad_maximum_fusion.6 = f32[32,64,128]{2,1,0:T(8,128)} fusion(f32[16,64,128]{2,1,0:T(8,128)S(1)} %copy-done.2, f32[16,64,128]{2,1,0:T(8,128)S(1)} %copy-done.3), kind=kLoop, calls=%fused_computation.21 | loop fusion | flops 262144 | bytes 2097152 | tf_op jit(solution)/shard_map/concatenate | solution.py:99
  24.3 0.8 copy-done.5
  25.8 1.1 %fusion.7 = f32[2,15,64,128]{3,2,1,0:T(8,128)} fusion(f32[1,16,64,128]{3,2,1,0:T(8,128)S(1)} %bitcast.70, f32[1,16,64,128]{3,2,1,0:T(8,128)S(1)} %bitcast.68, f32[15,64,128]{2,1,0:T(8,128)S(1)} %fusion.10), kind=kLoop, calls=%fused_computation.26 | loop fusion | flops 983040 | bytes 2523136 | tf_op jit(solution)/shard_map/mul | solution.py:156
  26.9 34.3 %all-reduce.2 = (f32[]{:T(128)}, f32[]{:T(128)}, f32[]{:T(128)}, f32[]{:T(128)}) all-reduce(f32[]{:T(128)} %get-tuple-element.3, f32[]{:T(128)} %get-tuple-element.4, f32[]{:T(128)} %get-tuple-element.5, f32[]{:T(128)} %get-tuple-element.2), channel_id=1, replica_groups=mesh['groups'=2,'gx'=4,'gy'=4] {'gx','gy'}, use_global_device_ids=true, to_apply=%region_5.0 | all-reduce | flops 4 | bytes 32 | tf_op jit(solution)/shard_map/psum | solution.py:70
  64.4 3.8 %copy.94 = f32[65,64,1]{2,1,0:T(8,128)} copy(f32[65,64,1]{0,1,2:T(8,128)} %collective-permute-done.1) | data formatting | bytes 33280 | tf_op jit(solution)/shard_map/ppermute | solution.py:33
  68.2 3.7 %copy.93 = f32[65,64,1]{2,1,0:T(8,128)} copy(f32[65,64,1]{0,1,2:T(8,128)} %collective-permute-done) | data formatting | bytes 33280 | tf_op jit(solution)/shard_map/ppermute | solution.py:31
  71.9 2.6 %pad_maximum_fusion = f32[32,64,130]{2,1,0:T(8,128)S(1)} fusion(f32[65,64,1]{2,1,0:T(8,128)} %copy.94, f32[65,64,128]{2,1,0:T(8,128)S(1)} %get-tuple-element.12, f32[65,64,1]{2,1,0:T(8,128)} %copy.93), kind=kLoop, calls=%fused_computation.1 | loop fusion | flops 532480 | bytes 3228160 | tf_op jit(solution)/shard_map/concatenate | solution.py:29
  75.8 2.1 %subtract_multiply_fusion = f32[2,16,64,129]{3,2,1,0:T(8,128)} fusion(f32[2,16,64,130]{3,2,1,0:T(8,128)S(1)} %bitcast.67, f32[16,64,129]{2,1,0:T(8,128)S(1)} %get-tuple-element.25, f32[16,64,129]{2,1,0:T(8,128)S(1)} %get-tuple-element.10, f32[16,64,129]{2,1,0:T(8,128)S(1)} %get-tuple-element.24), kind=kLoop, calls=%fused_computation.3 | loop fusion | flops 1849344 | bytes 4755456 | tf_op jit(solution)/shard_map/mul | solution.py:42
  78.0 1.1 %pad_maximum_fusion.3 = f32[32,65,128]{2,1,0:T(8,128)} fusion(f32[65,64,128]{2,1,0:T(8,128)S(1)} %get-tuple-element.12, f32[65,1,128]{2,1,0:T(1,128)S(1)} %collective-permute-done.6), kind=kLoop, calls=%fused_computation.9 | loop fusion | flops 266240 | bytes 3228160 | tf_op jit(solution)/shard_map/concatenate | solution.py:29
  80.8 1.0 %collective-permute-done.3 = f32[49,128]{1,0:T(8,128)S(1)} collective-permute-done((f32[49,128]{1,0:T(8,128)S(1)}, f32[49,128]{1,0:T(8,128)S(1)}, u32[]{:S(2)}, u32[]{:S(2)}) %collective-permute-start.3) | collective-permute-done | bytes 25120 | tf_op jit(solution)/shard_map/ppermute | solution.py:17
  81.8 1.8 %collective-permute-start.4 = (f32[49,128]{1,0:T(8,128)S(1)}, f32[49,128]{1,0:T(8,128)S(1)}, u32[]{:S(2)}, u32[]{:S(2)}) collective-permute-start(f32[49,128]{1,0:T(8,128)S(1)} %collective-permute-done.3), channel_id=1, source_target_pairs={{0,12},{4,0},{8,4},{12,8},{1,13},{5,1},{9,5},{13,9},{2,14},{6,2},{... | collective-permute-start | bytes 75272 | tf_op jit(solution)/shard_map/ppermute | solution.py:17
  83.6 2.1 %collective-permute-done.4 = f32[49,128]{1,0:T(8,128)S(1)} collective-permute-done((f32[49,128]{1,0:T(8,128)S(1)}, f32[49,128]{1,0:T(8,128)S(1)}, u32[]{:S(2)}, u32[]{:S(2)}) %collective-permute-start.4) | collective-permute-done | bytes 25120 | tf_op jit(solution)/shard_map/ppermute | solution.py:17
  88.7 1.3 %copy-done.4 = f32[2,16,64,129]{3,2,1,0:T(8,128)S(1)} copy-done((f32[2,16,64,129]{3,2,1,0:T(8,128)S(1)}, f32[2,16,64,129]{3,2,1,0:T(8,128)}, u32[]{:S(2)}) %copy-start.4) | copy-done | bytes 1056792
  91.0 0.8 slice_bitcast_fusion
  91.9 0.8 pad_maximum_fusion.9
  (93 shorter events, 9.0 us)
Async XLA Ops:
  0.6 2.4 %copy-start.10 = (f32[2,16,64,128]{3,2,1,0:T(8,128)S(1)}, f32[2,16,64,128]{3,2,1,0:T(8,128)}, u32[]{:S(2)}) copy-start(f32[2,16,64,128]{3,2,1,0:T(8,128)} %param.10) | copy-start | bytes 3145732
  0.6 2.5 %copy-start.12 = (s32[64,128]{1,0:T(8,128)S(1)}, s32[64,128]{1,0:T(8,128)}, u32[]{:S(2)}) copy-start(s32[64,128]{1,0:T(8,128)} %param.11) | copy-start | bytes 98308
  0.7 2.5 %copy-start.14 = (s32[64,128]{1,0:T(8,128)S(1)}, s32[64,128]{1,0:T(8,128)}, u32[]{:S(2)}) copy-start(s32[64,128]{1,0:T(8,128)} %param.12) | copy-start | bytes 98308
  1.8 3.9 %copy-start.2 = (f32[16,64,128]{2,1,0:T(8,128)S(1)}, f32[16,64,128]{2,1,0:T(8,128)}, u32[]{:S(2)}) copy-start(f32[16,64,128]{2,1,0:T(8,128)} %param.9) | copy-start | bytes 1572868
  1.8 3.9 %copy-start.3 = (f32[16,64,128]{2,1,0:T(8,128)S(1)}, f32[16,64,128]{2,1,0:T(8,128)}, u32[]{:S(2)}) copy-start(f32[16,64,128]{2,1,0:T(8,128)} %param.8) | copy-start | bytes 1572868
  3.2 74.7 %collective-permute-start.6 = (f32[65,1,128]{2,1,0:T(1,128)S(1)}, f32[65,1,128]{2,1,0:T(1,128)S(1)}, u32[]{:S(2)}, u32[]{:S(2)}) collective-permute-start(f32[65,1,128]{2,1,0:T(1,128)S(1)} %get-tuple-element.17), channel_id=1, source_target_pairs={{0,1},{1,2},{2,3},{4,5},{5,6},{6,7},{8,9},{9,10},{10,11},{12,13},{... | collective-permute-start | bytes 99848 | tf_op jit(solution)/shard_map/ppermute | solution.py:31
  6.4 71.5 %collective-permute-start.2 = (f32[49,128]{1,0:T(8,128)}, f32[49,128]{1,0:T(8,128)S(1)}, u32[]{:S(2)}, u32[]{:S(2)}) collective-permute-start(f32[49,128]{1,0:T(8,128)} %get-tuple-element.22), channel_id=1, source_target_pairs={{0,12},{4,0},{8,4},{12,8},{1,13},{5,1},{9,5},{13,9},{2,14},{6,2},{... | collective-permute-start | bytes 75272 | tf_op jit(solution)/shard_map/ppermute | solution.py:17
  10.8 68.3 %collective-permute-start.5 = (f32[65,1,128]{2,1,0:T(1,128)S(1)}, f32[65,1,128]{2,1,0:T(1,128)}, u32[]{:S(2)}, u32[]{:S(2)}) collective-permute-start(f32[65,1,128]{2,1,0:T(1,128)S(1)} %get-tuple-element.16), channel_id=1, source_target_pairs={{1,0},{2,1},{3,2},{5,4},{6,5},{7,6},{9,8},{10,9},{11,10},{13,12},{... | collective-permute-start | bytes 99848 | tf_op jit(solution)/shard_map/ppermute | solution.py:33
  14.9 8.2 %copy-start.16 = (s32[128]{0:T(128)S(1)}, s32[128]{0:T(128)}, u32[]{:S(2)}) copy-start(s32[128]{0:T(128)} %param.15) | copy-start | bytes 1540
  17.7 46.7 %collective-permute-start.1 = (f32[65,64,1]{0,1,2:T(8,128)S(1)}, f32[65,64,1]{0,1,2:T(8,128)}, u32[]{:S(2)}, u32[]{:S(2)}) collective-permute-start(f32[65,64,1]{0,1,2:T(8,128)S(1)} %copy.92), channel_id=1, source_target_pairs={{4,0},{8,4},{12,8},{0,12},{5,1},{9,5},{13,9},{1,13},{6,2},{10,6},{... | collective-permute-start | bytes 49928 | tf_op jit(solution)/shard_map/ppermute | solution.py:33
  21.5 3.6 %copy-start.15 = (f32[64,128]{1,0:T(8,128)S(1)}, f32[64,128]{1,0:T(8,128)}, u32[]{:S(2)}) copy-start(f32[64,128]{1,0:T(8,128)} %param.13) | copy-start | bytes 98308
  21.5 46.7 %collective-permute-start = (f32[65,64,1]{0,1,2:T(8,128)}, f32[65,64,1]{0,1,2:T(8,128)}, u32[]{:S(2)}, u32[]{:S(2)}) collective-permute-start(f32[65,64,1]{0,1,2:T(8,128)} %copy.91), channel_id=1, source_target_pairs={{0,4},{4,8},{8,12},{12,0},{1,5},{5,9},{9,13},{13,1},{2,6},{6,10},{... | collective-permute-start | bytes 49928 | tf_op jit(solution)/shard_map/ppermute | solution.py:31
  23.1 2.0 %copy-start.11 = (f32[64,128]{1,0:T(8,128)S(1)}, f32[64,128]{1,0:T(8,128)}, u32[]{:S(2)}) copy-start(f32[64,128]{1,0:T(8,128)} %param.14) | copy-start | bytes 98308
  24.2 0.8 copy-start.5
  71.9 2.6 %copy-start = (f32[65,64,1]{2,1,0:T(8,128)S(1)}, f32[65,64,1]{2,1,0:T(8,128)}, u32[]{:S(2)}) copy-start(f32[65,64,1]{2,1,0:T(8,128)} %copy.93) | copy-start | bytes 49924
  71.9 2.9 %copy-start.1 = (f32[65,64,1]{2,1,0:T(8,128)S(1)}, f32[65,64,1]{2,1,0:T(8,128)}, u32[]{:S(2)}) copy-start(f32[65,64,1]{2,1,0:T(8,128)} %copy.94) | copy-start | bytes 49924
  75.8 2.2 %copy-start.13 = (f32[49,1024]{1,0:T(8,128)S(1)}, f32[49,1024]{1,0:T(8,128)}, u32[]{:S(2)}) copy-start(f32[49,1024]{1,0:T(8,128)} %get-tuple-element.23) | copy-start | bytes 602116
  77.9 3.9 %collective-permute-start.3 = (f32[49,128]{1,0:T(8,128)S(1)}, f32[49,128]{1,0:T(8,128)S(1)}, u32[]{:S(2)}, u32[]{:S(2)}) collective-permute-start(f32[49,128]{1,0:T(8,128)S(1)} %collective-permute-done.2), channel_id=1, source_target_pairs={{0,12},{4,0},{8,4},{12,8},{1,13},{5,1},{9,5},{13,9},{2,14},{6,2},{... | collective-permute-start | bytes 75272 | tf_op jit(solution)/shard_map/ppermute | solution.py:17
  81.8 3.9 %collective-permute-start.4 = (f32[49,128]{1,0:T(8,128)S(1)}, f32[49,128]{1,0:T(8,128)S(1)}, u32[]{:S(2)}, u32[]{:S(2)}) collective-permute-start(f32[49,128]{1,0:T(8,128)S(1)} %collective-permute-done.3), channel_id=1, source_target_pairs={{0,12},{4,0},{8,4},{12,8},{1,13},{5,1},{9,5},{13,9},{2,14},{6,2},{... | collective-permute-start | bytes 75272 | tf_op jit(solution)/shard_map/ppermute | solution.py:17
  86.8 1.3 %copy-start.7 = (f32[32,65,128]{2,1,0:T(8,128)S(1)}, f32[32,65,128]{2,1,0:T(8,128)}, u32[]{:S(2)}) copy-start(f32[32,65,128]{2,1,0:T(8,128)} %pad_maximum_fusion.3) | copy-start | bytes 3194884
  86.8 1.6 %copy-start.8 = (f32[32,64,128]{2,1,0:T(8,128)S(1)}, f32[32,64,128]{2,1,0:T(8,128)}, u32[]{:S(2)}) copy-start(f32[32,64,128]{2,1,0:T(8,128)} %pad_maximum_fusion.6) | copy-start | bytes 3145732
  88.4 1.6 %copy-start.4 = (f32[2,16,64,129]{3,2,1,0:T(8,128)S(1)}, f32[2,16,64,129]{3,2,1,0:T(8,128)}, u32[]{:S(2)}) copy-start(f32[2,16,64,129]{3,2,1,0:T(8,128)} %subtract_multiply_fusion) | copy-start | bytes 3170308
  88.4 1.7 %copy-start.6 = (f32[16,64,128]{2,1,0:T(8,128)S(1)}, f32[16,64,128]{2,1,0:T(8,128)}, u32[]{:S(2)}) copy-start(f32[16,64,128]{2,1,0:T(8,128)} %copy-done.5) | copy-start | bytes 1572868
  88.4 2.0 %copy-start.9 = (f32[2,15,64,128]{3,2,1,0:T(8,128)S(1)}, f32[2,15,64,128]{3,2,1,0:T(8,128)}, u32[]{:S(2)}) copy-start(f32[2,15,64,128]{3,2,1,0:T(8,128)} %fusion.7) | copy-start | bytes 2949124
